TPU v7x, 512 devices: a 8x2x16 block of a 8x8x16 slice. The times are simulated.
512 devices in a mesh: job: 2 (over y), row: 16 (over z), col: 8 (over x), samp: 2 (over core).
Axes of the slice: x: 8, y: 2, z: 16, core: 2. Of those that a mesh axis runs over, the one named last changes fastest.
The devices are a block of a 8x8x16 slice.
Arguments:
- pair_repr: bfloat16 [1024, 512, 128], P(('job', 'row'), ('col', 'samp')), parts along dimension 0, may hold values from -100 to 100
- asym_id: int32 [1024], P('job'), parts along dimension 0, may hold values from 0 to 7, never falling along the last dimension, each value on 1 to 128 neighbouring positions
- valid_len: int32 [2], P('job'), parts along dimension 0, may hold values from 256 to 512
- rel_embed: bfloat16 [128, 128], replicated, may hold values from -12 to 12
- pair_gain: float32 [128], replicated, may hold values from 0.25 to 1.75
- bias_weight: bfloat16 [128, 16], replicated, may hold values from -64 to 64
- tokens: bfloat16 [128, 512, 768], P(('job', 'col', 'samp'), 'row'), parts along dimension 0, may hold values from -6 to 6
- token_gain: float32 [1, 768], replicated, may hold values from 0.25 to 1.75
- qkv_weight: bfloat16 [1, 3, 768, 768], P(None, None, None, 'row'), may hold values from -0.21875 to 0.21875
- out_weight: bfloat16 [1, 768, 768], P(None, 'row'), may hold values from -0.21875 to 0.21875
Outputs:
- refined: bfloat16 [128, 512, 768], P(('job', 'col', 'samp'), 'row'), parts along dimension 0
There are 2 independent parts, one for each index of `job`. A program takes and returns all parts, laid end to end along the dimension named above; an argument that names none is the same for every part. Nothing has to cross between parts.
Inputs may be any that keep to these rules, and one draw needn't show every extreme that they name: `asym_id`: chain indices never fall along the tokens.
All inputs are finite; a program needn't handle non-finite values.
Results may differ from a plain program's by a relative error of at most 0.002.
The roundings to bfloat16 on the way count: a program that leaves them out, or rounds other values in their place, can miss the bound.
Values may be sent and summed in bfloat16 or wider, within the bound.
No kernel may reach another device: no remote copies, remote signals or barrier semaphores. Data moves between devices by JAX's collectives and lax.ppermute only.
A program may use at most 64 MiB of HBM per device.

v0:
```python
import math
import jax
import jax.numpy as jnp
from jax import lax
from jax.sharding import PartitionSpec as P

HEAD_DIM = 48
epsilon = 1e-05


def joined_along(tiles, dim):
    dims = list(tiles.shape[1:])
    dims[dim] *= tiles.shape[0]
    return jnp.moveaxis(tiles, 0, dim).reshape(dims)


def from_everyone(shard, axis):
    copies = jnp.broadcast_to(shard, (lax.axis_size(axis), *shard.shape))
    return lax.all_to_all(copies, axis, split_axis=0, concat_axis=0, tiled=True)


def gathered_copies(shard, axis, dim):
    return joined_along(from_everyone(shard, axis), dim)


def normalize(values, gain_vector):
    average = jnp.mean(values, axis=-1, keepdims=True)
    centered = values - average
    variance = jnp.mean(centered * centered, axis=-1, keepdims=True)
    return centered * lax.rsqrt(variance + epsilon) * gain_vector


def bias_tile_of(pair_repr, asym_id, rel_embed, pair_gain, bias_weight):
    tile_rows, tile_cols, channels = pair_repr.shape
    bin_count = rel_embed.shape[0]
    reach_max = bin_count // 2 - 1
    first_row = lax.axis_index("row") * tile_rows
    first_col = lax.axis_index(("col", "samp")) * tile_cols
    row_ids = first_row + jnp.arange(tile_rows, dtype=jnp.int32)
    col_ids = first_col + jnp.arange(tile_cols, dtype=jnp.int32)
    row_chain = lax.dynamic_slice_in_dim(asym_id, first_row, tile_rows, 0)
    col_chain = lax.dynamic_slice_in_dim(asym_id, first_col, tile_cols, 0)
    offset = jnp.clip(row_ids[:, None] - col_ids[None, :], -reach_max, reach_max) + reach_max
    bin_ids = jnp.where(row_chain[:, None] == col_chain[None, :], offset, bin_count - 1)
    onehot = (
        bin_ids.reshape(-1)[:, None] == jnp.arange(bin_count, dtype=jnp.int32)[None, :]
    ).astype(jnp.bfloat16)
    summed = pair_repr.reshape(-1, channels).astype(jnp.float32) + jnp.dot(
        onehot, rel_embed, preferred_element_type=jnp.float32
    )
    normed = normalize(summed, pair_gain).astype(jnp.bfloat16)
    projected = lax.dot_general(
        bias_weight, normed, (((0,), (1,)), ((), ())), preferred_element_type=jnp.float32
    )
    return projected.reshape(bias_weight.shape[1], tile_rows, tile_cols)


def attend(queries, key_rows, value_rows, pair_bias, keymask, score_scale):
    head_count, query_count, key_count = pair_bias.shape
    model_width = queries.shape[-1]
    head_width = model_width // head_count
    query_h = queries.reshape(query_count, head_count, head_width)
    key_h = key_rows.reshape(key_count, head_count, head_width)
    value_h = value_rows.reshape(key_count, head_count, head_width)
    scores = (
        jnp.einsum("ihd,jhd->hij", query_h, key_h, preferred_element_type=jnp.float32) * score_scale
        + pair_bias
    )
    scores = jnp.where(keymask[None, None, :], scores, -1e30)
    row_max = jnp.max(scores, axis=-1, keepdims=True)
    weights = jnp.where(keymask[None, None, :], jnp.exp(scores - row_max), 0.0)
    row_total = jnp.sum(weights, axis=-1, keepdims=True)
    probs = (weights / row_total).astype(jnp.bfloat16)
    attended = jnp.einsum("hij,jhd->ihd", probs, value_h, preferred_element_type=jnp.float32)
    return attended.reshape(query_count, model_width).astype(jnp.bfloat16)


def per_device(
    pair_repr,
    asym_id,
    valid_len,
    rel_embed,
    pair_gain,
    bias_weight,
    tokens,
    token_gain,
    qkv_weight,
    out_weight,
):
    sample_count, token_rows, model_width = tokens.shape
    total_tokens = asym_id.shape[0]
    keymask = jnp.arange(total_tokens, dtype=jnp.int32) < valid_len[0]
    score_scale = 1.0 / math.sqrt(HEAD_DIM)
    bias_tile = bias_tile_of(pair_repr, asym_id, rel_embed, pair_gain, bias_weight)
    head_tile = lax.all_to_all(bias_tile, "row", split_axis=0, concat_axis=1, tiled=True)
    pair_bias = gathered_copies(head_tile, ("col", "samp"), 2)

    def one_sample(sample_item):
        return attend(
            sample_item[0], sample_item[1], sample_item[2], pair_bias, keymask, score_scale
        )

    current = tokens
    normed = normalize(current.astype(jnp.float32), token_gain[0]).astype(jnp.bfloat16)
    layer_weight = qkv_weight[0]
    projected = jnp.einsum(
        "snc,pcw->psnw",
        lax.all_gather(normed, "row", axis=1, tiled=True),
        layer_weight,
        preferred_element_type=jnp.float32,
    ).astype(jnp.bfloat16)
    head_out = lax.map(one_sample, (projected[0], projected[1], projected[2]))
    attended = lax.all_to_all(head_out, "row", split_axis=1, concat_axis=2, tiled=True)
    flattened = attended.reshape(sample_count * token_rows, model_width)
    update = jnp.dot(
        flattened, gathered_copies(out_weight[0], "row", 0), preferred_element_type=jnp.float32
    )
    current = (
        current.astype(jnp.float32) + update.reshape(sample_count, token_rows, model_width)
    ).astype(jnp.bfloat16)
    return current


def solution(mesh):
    return jax.shard_map(
        per_device,
        mesh=mesh,
        in_specs=(
            P(("job", "row"), ("col", "samp"), None),
            P("job"),
            P("job"),
            P(),
            P(),
            P(),
            P(("job", "col", "samp"), "row", None),
            P(),
            P(None, None, None, "row"),
            P(None, "row", None),
        ),
        out_specs=P(("job", "col", "samp"), "row", None),
        check_vma=False,
    )
```

profile of v0, /device:TPU:66, one launch (start us, length us, event | category | flops | bytes accessed | tf_op | source)
XLA Modules:
  0.0 212.2 jit_solution(4686499185839951413)
XLA Ops:
  6.6 1.1 convert_reduce_fusion
  7.7 1.1 fusion.31
  8.8 0.7 reduce.4
  9.5 1.8 fusion.33
  11.4 0.8 fusion.40
  12.2 0.1 add_select_fusion
  12.3 0.1 select_n.29
  12.4 0.2 copy.23
  12.7 1.0 fusion.41
  13.6 0.1 multiply_reduce_fusion
  13.7 0.2 convolution_bitcast_fusion.1
  14.0 0.1 reshape.153
  14.1 0.2 reshape.165
  14.2 56.2 %all_to_all.37 = f32[16,1,1024]{2,1,0:T(1,128)S(1)} all-to-all(f32[16,1,1024]{2,1,0:T(1,128)S(1)} %reshape.165), channel_id=1, replica_groups=mesh['job'=2,'row'=16,'col'=8,'samp'=2] {'row'}, dimensions={0} | all-to-all | bytes 131072 | tf_op jit(solution)/shard_map/all_to_all | solution.py:95
  70.4 0.5 broadcast.109
  70.9 0.7 reduce.5
  71.6 0.1 reshape.166
  71.7 0.1 copy.24
  71.8 1.1 broadcast_in_dim.49
  72.9 7.7 %all-to-all-start.1 = ((f32[16,1,512,32]{2,3,1,0:T(8,128)}), f32[16,1,512,32]{2,3,1,0:T(8,128)S(1)}, u32[]{:S(2)}, u32[]{:S(2)}) async-start(f32[16,1,512,32]{2,3,1,0:T(8,128)} %broadcast_in_dim.49), calls=%async_computation.1 | async-start | bytes 2097152 | tf_op jit(solution)/shard_map/all_to_all | solution.py:19
  80.7 42.3 %all-gather.2.cloned.1.call-done = bf16[4,512,768]{2,1,0:T(8,128)(2,1)} async-done(((bf16[4,32,768]{2,1,0:T(8,128)(2,1)}), bf16[4,512,768]{2,1,0:T(8,128)(2,1)}) %all-gather.2.cloned.1.call-update) | async-done | bytes 3145744 | tf_op jit(solution)/shard_map/all_gather | solution.py:108
  122.9 3.0 %fusion.21 = bf16[3,4,512,48]{2,3,0,1:T(8,128)(2,1)S(1)} fusion(bf16[4,512,768]{2,1,0:T(8,128)(2,1)} %all-gather.2.cloned.1.call-done, bf16[1,3,768,48]{2,3,1,0:T(8,128)(2,1)S(1)} %copy-done), kind=kOutput, calls=%fused_computation.23 | convolution fusion | flops 453279744 | bytes 3956736 | tf_op jit(solution)/shard_map/snc,pcw->psnw/dot_general | solution.py:106
  126.1 6.6 %while.11 = (s32[]{:T(128)}, bf16[4,512,48]{1,2,0:T(8,128)(2,1)S(1)}, bf16[4,512,48]{1,2,0:T(8,128)(2,1)S(1)}, bf16[4,512,48]{1,2,0:T(8,128)(2,1)S(1)}, bf16[4,5...) while((s32[]{:T(128)}, bf16[4,512,48]{1,2,0:T(8,128)(2,1)S(1)}, ...), condition=%wide.region_7.8_spmd.clone, body=%wide.region_4.7_spmd.clone.sunk | while | flops 53239296 | bytes 4405345 | solution.py:112
  126.1 0.7 iota_compare_fusion.4
  126.7 0.4 fusion.50
  127.1 0.2 fusion.51
  127.3 0.4 fusion.52
  127.7 0.7 iota_compare_fusion.4
  128.4 0.4 fusion.50
  128.8 0.2 fusion.51
  129.0 0.4 fusion.52
  129.4 0.7 iota_compare_fusion.4
  130.0 0.4 fusion.50
  130.4 0.2 fusion.51
  130.6 0.4 fusion.52
  131.0 0.7 iota_compare_fusion.4
  131.7 0.4 fusion.50
  132.1 0.2 fusion.51
  132.3 0.4 fusion.52
  132.7 0.3 copy.28
  133.0 0.8 reshape.167
  133.8 21.0 %all_to_all.38 = bf16[16,2,3072]{2,1,0:T(2,128)(2,1)S(1)} all-to-all(bf16[16,2,3072]{2,1,0:T(2,128)(2,1)S(1)} %reshape.167), channel_id=1, replica_groups=mesh['job'=2,'row'=16,'col'=8,'samp'=2] {'row'}, dimensions={0} | all-to-all | bytes 393216 | tf_op jit(solution)/shard_map/all_to_all | solution.py:113
  154.7 1.1 broadcast_in_dim.50
  155.8 5.2 %all-to-all-start.3 = ((bf16[16,48,768]{2,1,0:T(8,128)(2,1)}), bf16[16,48,768]{2,1,0:T(8,128)(2,1)S(1)}, u32[]{:S(2)}, u32[]{:S(2)}) async-start(bf16[16,48,768]{2,1,0:T(8,128)(2,1)} %broadcast_in_dim.50), calls=%async_computation.3 | async-start | bytes 2359296 | tf_op jit(solution)/shard_map/all_to_all | solution.py:19
  161.0 0.5 reshape.168
  161.6 0.1 copy.29
  161.7 42.5 %all-to-all-done.3 = bf16[16,48,768]{2,1,0:T(8,128)(2,1)S(1)} async-done(((bf16[16,48,768]{2,1,0:T(8,128)(2,1)}), bf16[16,48,768]{2,1,0:T(8,128)(2,1)S(1)}, u32[]{:S(2)}, u32[]{:S(2)}) %all-to-all-start.3) | async-done | bytes 1179680 | tf_op jit(solution)/shard_map/all_to_all | solution.py:19
  204.2 1.1 fusion.26
  (25 shorter events, 0.2 us)
Async XLA Ops:
  6.5 116.4 %copy-start = (bf16[1,3,768,48]{2,3,1,0:T(8,128)(2,1)S(1)}, bf16[1,3,768,48]{2,3,1,0:T(8,128)(2,1)}, u32[]{:S(2)}) copy-start(bf16[1,3,768,48]{2,3,1,0:T(8,128)(2,1)} %param.20) | copy-start | bytes 663556
  6.6 5.8 %copy-start.2 = (bf16[32,32,128]{2,1,0:T(8,128)(2,1)S(1)}, bf16[32,32,128]{2,1,0:T(8,128)(2,1)}, u32[]{:S(2)}) copy-start(bf16[32,32,128]{2,1,0:T(8,128)(2,1)} %param.12) | copy-start | bytes 786436
  6.6 116.4 %all-gather.2.cloned.1.call-start = ((), (), s32[]{:S(2)}) async-start(), calls=%async_computation.4 | async-start | bytes 3342336 | tf_op jit(solution)/shard_map/all_gather | solution.py:108
  9.5 3.1 %copy-start.4 = (bf16[128,128]{1,0:T(8,128)(2,1)S(1)}, bf16[128,128]{1,0:T(8,128)(2,1)}, u32[]{:S(2)}) copy-start(bf16[128,128]{1,0:T(8,128)(2,1)} %param.15) | copy-start | bytes 98308
  12.4 1.3 copy-start.5
  12.4 1.3 copy-start.6
  72.9 53.1 %all-to-all-start.1 = ((f32[16,1,512,32]{2,3,1,0:T(8,128)}), f32[16,1,512,32]{2,3,1,0:T(8,128)S(1)}, u32[]{:S(2)}, u32[]{:S(2)}) async-start(f32[16,1,512,32]{2,3,1,0:T(8,128)} %broadcast_in_dim.49), calls=%async_computation.1 | async-start | bytes 2097152 | tf_op jit(solution)/shard_map/all_to_all | solution.py:19
  132.6 22.1 %copy-start.3 = (bf16[1,48,768]{2,1,0:T(8,128)(2,1)S(1)}, bf16[1,48,768]{2,1,0:T(8,128)(2,1)}, u32[]{:S(2)}) copy-start(bf16[1,48,768]{2,1,0:T(8,128)(2,1)} %param.21) | copy-start | bytes 221188
  155.8 48.3 %all-to-all-start.3 = ((bf16[16,48,768]{2,1,0:T(8,128)(2,1)}), bf16[16,48,768]{2,1,0:T(8,128)(2,1)S(1)}, u32[]{:S(2)}, u32[]{:S(2)}) async-start(bf16[16,48,768]{2,1,0:T(8,128)(2,1)} %broadcast_in_dim.50), calls=%async_computation.3 | async-start | bytes 2359296 | tf_op jit(solution)/shard_map/all_to_all | solution.py:19
  161.0 43.1 %copy-start.1 = (bf16[4,32,768]{2,1,0:T(8,128)(2,1)S(1)}, bf16[4,32,768]{2,1,0:T(8,128)(2,1)}, u32[]{:S(2)}) copy-start(bf16[4,32,768]{2,1,0:T(8,128)(2,1)} %param.18) | copy-start | bytes 589828
Sparse Core Ops, SparseCore 0:
  11.5 111.4 all-gather.1
where the time goes:
time: 213 us; the launch traced here: 212 us
  waiting for transfers between devices  84.9 us (40%)
  blocking collectives  77.1 us (36%)
  between operations  13.7 us (6%)
  starting transfers between devices  12.9 us (6%)
  other arithmetic  9.07 us (4%)
  matrix products  8.32 us (4%)
  local copies, waits for them, and re-layouts  6.06 us (3%)
    all_to_all x1, blocking collectives, per_device(): lax.all_to_all(bias_tile, 'row', split_axis=0, concat_axis=1, tiled=True)  56.2 us
    all_to_all x2, waiting for transfers between devices, from_everyone(): return lax.all_to_all(copies, axis, split_axis=0, concat_axis=0, tiled=True)  42.5 us
    all_gather x1, waiting for transfers between devices, per_device(): lax.all_gather(normed, 'row', axis=1, tiled=True)  42.3 us
    all_to_all x1, blocking collectives, per_device(): lax.all_to_all(head_out, 'row', split_axis=1, concat_axis=2, tiled=True)  21 us
    all_to_all x2, starting transfers between devices, from_everyone(): return lax.all_to_all(copies, axis, split_axis=0, concat_axis=0, tiled=True)  12.9 us
  transfers between devices with their start and end apart: 3, of which 2 were waited for; matrix products, arithmetic and copies ran while one was open for 4% of the time, Pallas kernels for 0%

commit v1 on v0

--- a/solution.py
+++ b/solution.py
@@ -105,7 +105,9 @@
     layer_weight = qkv_weight[0]
     projected = jnp.einsum(
         "snc,pcw->psnw",
-        lax.all_gather(normed, "row", axis=1, tiled=True),
+        jnp.concatenate(
+            lax.all_to_all(jnp.stack([normed] * lax.axis_size("row")), "row", 0, 0), axis=1
+        ),
         layer_weight,
         preferred_element_type=jnp.float32,
     ).astype(jnp.bfloat16)

time: 213 us -> 338 us (1.59)
  the two profiles are of different devices: /device:TPU:66 before, /device:TPU:80 now
where the time goes in v1:
time: 338 us; the launch traced here: 337 us
  waiting for transfers between devices  224 us (66%)
  starting transfers between devices  63.4 us (19%)
  blocking collectives  22.9 us (7%)
  local copies, waits for them, and re-layouts  13.5 us (4%)
  matrix products  6.66 us (2%)
  other arithmetic  6.02 us (2%)
    all_to_all x1, waiting for transfers between devices, per_device(): lax.all_to_all(jnp.stack([normed] * lax.axis_size('row')), 'row', 0, 0)  135 us
    all_to_all x2, waiting for transfers between devices, from_everyone(): return lax.all_to_all(copies, axis, split_axis=0, concat_axis=0, tiled=True)  77.3 us
    all_to_all x1, starting transfers between devices, per_device(): lax.all_to_all(bias_tile, 'row', split_axis=0, concat_axis=1, tiled=True)  43.7 us
    all_to_all x1, blocking collectives, per_device(): lax.all_to_all(head_out, 'row', split_axis=1, concat_axis=2, tiled=True)  22.9 us
    all_to_all x2, starting transfers between devices, from_everyone(): return lax.all_to_all(copies, axis, split_axis=0, concat_axis=0, tiled=True)  15.6 us
    all_to_all x1, waiting for transfers between devices, per_device(): lax.all_to_all(bias_tile, 'row', split_axis=0, concat_axis=1, tiled=True)  12.1 us
  transfers between devices with their start and end apart: 4, of which 4 were waited for; matrix products, arithmetic and copies ran while one was open for 2% of the time, Pallas kernels for 0%

profile of v1, /device:TPU:80, one launch (start us, length us, event | category | flops | bytes accessed | tf_op | source)
XLA Modules:
  0.0 337.2 jit_solution(3251617102425778588)
XLA Ops:
  0.1 1.1 bitcast_convert_fusion
  1.1 0.2 copy.24
  1.4 0.8 fusion.33
  2.3 1.2 fusion.34
  3.6 0.2 convolution_bitcast_fusion.1
  4.0 0.8 reshape.175
  4.8 43.7 %all-to-all-start.1 = ((f32[16,1,1024]{2,1,0:T(1,128)}), f32[16,1,1024]{2,1,0:T(1,128)S(1)}, u32[]{:S(2)}, u32[]{:S(2)}) async-start(f32[16,1,1024]{2,1,0:T(1,128)} %reshape.175), calls=%async_computation.1 | async-start | bytes 131072 | tf_op jit(solution)/shard_map/all_to_all | solution.py:95
  48.6 0.2 fusion.24
  48.9 0.1 fusion.26
  49.0 12.1 %all-to-all-done.1 = f32[16,1,1024]{2,1,0:T(1,128)S(1)} async-done(((f32[16,1,1024]{2,1,0:T(1,128)}), f32[16,1,1024]{2,1,0:T(1,128)S(1)}, u32[]{:S(2)}, u32[]{:S(2)}) %all-to-all-start.1) | async-done | bytes 65568 | tf_op jit(solution)/shard_map/all_to_all | solution.py:95
  61.2 2.1 stack.2
  63.2 4.2 %all-to-all-start = ((bf16[16,4,32,768]{3,2,1,0:T(8,128)(2,1)}), bf16[16,4,32,768]{3,2,1,0:T(8,128)(2,1)S(1)}, u32[]{:S(2)}, u32[]{:S(2)}) async-start(bf16[16,4,32,768]{3,2,1,0:T(8,128)(2,1)} %stack.2), calls=%async_computation | async-start | bytes 6291456 | tf_op jit(solution)/shard_map/all_to_all | solution.py:109
  67.4 0.5 broadcast.111
  67.9 0.8 reduce.5
  68.7 0.8 reshape.176
  69.6 1.0 copy.25
  70.6 134.9 %all-to-all-done = bf16[16,4,32,768]{3,2,1,0:T(8,128)(2,1)S(1)} async-done(((bf16[16,4,32,768]{3,2,1,0:T(8,128)(2,1)}), bf16[16,4,32,768]{3,2,1,0:T(8,128)(2,1)S(1)}, u32[]{:S(2)}, u32[]{:S(2)}) %all-to-all-start) | async-done | bytes 3145760 | tf_op jit(solution)/shard_map/all_to_all | solution.py:109
  205.5 1.2 broadcast_in_dim.49
  206.7 0.8 copy-done.1
  207.5 7.6 %all-to-all-start.2 = ((f32[16,1,512,32]{2,3,1,0:T(8,128)}), f32[16,1,512,32]{2,3,1,0:T(8,128)S(1)}, u32[]{:S(2)}, u32[]{:S(2)}) async-start(f32[16,1,512,32]{2,3,1,0:T(8,128)} %broadcast_in_dim.49), calls=%async_computation.2 | async-start | bytes 2097152 | tf_op jit(solution)/shard_map/all_to_all | solution.py:19
  215.1 2.2 copy.23
  217.3 1.2 fusion.16
  218.5 22.9 %all-to-all-done.2 = f32[16,1,512,32]{2,3,1,0:T(8,128)S(1)} async-done(((f32[16,1,512,32]{2,3,1,0:T(8,128)}), f32[16,1,512,32]{2,3,1,0:T(8,128)S(1)}, u32[]{:S(2)}, u32[]{:S(2)}) %all-to-all-start.2) | async-done | bytes 1048608 | tf_op jit(solution)/shard_map/all_to_all | solution.py:19
  241.4 6.6 %while.11 = (s32[]{:T(128)}, bf16[4,512,48]{1,2,0:T(8,128)(2,1)S(1)}, bf16[4,512,48]{1,2,0:T(8,128)(2,1)S(1)}, bf16[4,512,48]{1,2,0:T(8,128)(2,1)S(1)}, bf16[4,5...) while((s32[]{:T(128)}, bf16[4,512,48]{1,2,0:T(8,128)(2,1)S(1)}, ...), condition=%wide.region_7.8_spmd.clone, body=%wide.region_4.7_spmd.clone.sunk | while | flops 53239296 | bytes 4405345 | solution.py:114
  241.4 0.7 iota_compare_fusion.4
  242.1 0.4 fusion.44
  242.5 0.2 fusion.45
  242.7 0.4 fusion.46
  243.1 0.7 iota_compare_fusion.4
  243.7 0.4 fusion.44
  244.1 0.2 fusion.45
  244.3 0.4 fusion.46
  244.7 0.7 iota_compare_fusion.4
  245.4 0.4 fusion.44
  245.8 0.2 fusion.45
  246.0 0.4 fusion.46
  246.4 0.7 iota_compare_fusion.4
  247.0 0.4 fusion.44
  247.4 0.2 fusion.45
  247.6 0.4 fusion.46
  248.0 0.3 copy.29
  248.3 0.8 reshape.177
  249.1 22.9 %all_to_all.42 = bf16[16,2,3072]{2,1,0:T(2,128)(2,1)S(1)} all-to-all(bf16[16,2,3072]{2,1,0:T(2,128)(2,1)S(1)} %reshape.177), channel_id=1, replica_groups=mesh['job'=2,'row'=16,'col'=8,'samp'=2] {'row'}, dimensions={0} | all-to-all | bytes 393216 | tf_op jit(solution)/shard_map/all_to_all | solution.py:115
  272.0 1.1 broadcast_in_dim.50
  273.1 7.9 %all-to-all-start.4 = ((bf16[16,48,768]{2,1,0:T(8,128)(2,1)}), bf16[16,48,768]{2,1,0:T(8,128)(2,1)S(1)}, u32[]{:S(2)}, u32[]{:S(2)}) async-start(bf16[16,48,768]{2,1,0:T(8,128)(2,1)} %broadcast_in_dim.50), calls=%async_computation.4 | async-start | bytes 2359296 | tf_op jit(solution)/shard_map/all_to_all | solution.py:19
  281.0 0.5 reshape.178
  281.6 54.5 %all-to-all-done.4 = bf16[16,48,768]{2,1,0:T(8,128)(2,1)S(1)} async-done(((bf16[16,48,768]{2,1,0:T(8,128)(2,1)}), bf16[16,48,768]{2,1,0:T(8,128)(2,1)S(1)}, u32[]{:S(2)}, u32[]{:S(2)}) %all-to-all-start.4) | async-done | bytes 1179680 | tf_op jit(solution)/shard_map/all_to_all | solution.py:19
  336.1 1.1 fusion.19
  (29 shorter events, 0.6 us)
Async XLA Ops:
  0.0 217.3 %copy-start = (bf16[1,3,768,48]{2,3,1,0:T(8,128)(2,1)S(1)}, bf16[1,3,768,48]{2,3,1,0:T(8,128)(2,1)}, u32[]{:S(2)}) copy-start(bf16[1,3,768,48]{2,3,1,0:T(8,128)(2,1)} %param.20) | copy-start | bytes 663556
  0.0 3.6 %copy-start.5 = (bf16[128,16]{0,1:T(8,128)(2,1)S(1)}, bf16[128,16]{0,1:T(8,128)(2,1)}, u32[]{:S(2)}) copy-start(bf16[128,16]{0,1:T(8,128)(2,1)} %param.17) | copy-start | bytes 12292
  0.0 3.6 %copy-start.7 = (f32[128]{0:T(128)S(1)}, f32[128]{0:T(128)}, u32[]{:S(2)}) copy-start(f32[128]{0:T(128)} %param.16) | copy-start | bytes 1540
  0.0 48.5 %copy-start.2 = (bf16[4,32,768]{2,1,0:T(8,128)(2,1)S(1)}, bf16[4,32,768]{2,1,0:T(8,128)(2,1)}, u32[]{:S(2)}) copy-start(bf16[4,32,768]{2,1,0:T(8,128)(2,1)} %param.18) | copy-start | bytes 589828
  0.0 48.8 %copy-start.6 = (f32[1,768]{1,0:T(1,128)S(1)}, f32[1,768]{1,0:T(1,128)}, u32[]{:S(2)}) copy-start(f32[1,768]{1,0:T(1,128)} %param.19) | copy-start | bytes 9220
  4.8 56.4 %all-to-all-start.1 = ((f32[16,1,1024]{2,1,0:T(1,128)}), f32[16,1,1024]{2,1,0:T(1,128)S(1)}, u32[]{:S(2)}, u32[]{:S(2)}) async-start(f32[16,1,1024]{2,1,0:T(1,128)} %reshape.175), calls=%async_computation.1 | async-start | bytes 131072 | tf_op jit(solution)/shard_map/all_to_all | solution.py:95
  63.2 142.3 %all-to-all-start = ((bf16[16,4,32,768]{3,2,1,0:T(8,128)(2,1)}), bf16[16,4,32,768]{3,2,1,0:T(8,128)(2,1)S(1)}, u32[]{:S(2)}, u32[]{:S(2)}) async-start(bf16[16,4,32,768]{3,2,1,0:T(8,128)(2,1)} %stack.2), calls=%async_computation | async-start | bytes 6291456 | tf_op jit(solution)/shard_map/all_to_all | solution.py:109
  205.5 2.0 copy-start.1
  207.5 33.9 %all-to-all-start.2 = ((f32[16,1,512,32]{2,3,1,0:T(8,128)}), f32[16,1,512,32]{2,3,1,0:T(8,128)S(1)}, u32[]{:S(2)}, u32[]{:S(2)}) async-start(f32[16,1,512,32]{2,3,1,0:T(8,128)} %broadcast_in_dim.49), calls=%async_computation.2 | async-start | bytes 2097152 | tf_op jit(solution)/shard_map/all_to_all | solution.py:19
  241.4 30.6 %copy-start.4 = (bf16[1,48,768]{2,1,0:T(8,128)(2,1)S(1)}, bf16[1,48,768]{2,1,0:T(8,128)(2,1)}, u32[]{:S(2)}) copy-start(bf16[1,48,768]{2,1,0:T(8,128)(2,1)} %param.21) | copy-start | bytes 221188
  248.3 87.8 %copy-start.3 = (bf16[4,32,768]{2,1,0:T(8,128)(2,1)S(1)}, bf16[4,32,768]{2,1,0:T(8,128)(2,1)}, u32[]{:S(2)}) copy-start(bf16[4,32,768]{2,1,0:T(8,128)(2,1)} %param.18) | copy-start | bytes 589828
  273.1 63.0 %all-to-all-start.4 = ((bf16[16,48,768]{2,1,0:T(8,128)(2,1)}), bf16[16,48,768]{2,1,0:T(8,128)(2,1)S(1)}, u32[]{:S(2)}, u32[]{:S(2)}) async-start(bf16[16,48,768]{2,1,0:T(8,128)(2,1)} %broadcast_in_dim.50), calls=%async_computation.4 | async-start | bytes 2359296 | tf_op jit(solution)/shard_map/all_to_all | solution.py:19
